TPU v7x, 512 devices: a 4x2x32 block of a 4x16x32 slice. The times are simulated.
512 devices in a mesh: groups: 2 (over y), row: 32 (over z), col: 4 (over x), sub: 2 (over core).
Axes of the slice: x: 4, y: 2, z: 32, core: 2. Of those that a mesh axis runs over, the one named last changes fastest.
The devices are a block of a 4x16x32 slice.
Arguments:
- matrix: float32 [16384, 8192], P(('groups', 'row'), ('col', 'sub')), parts along dimension 0, may hold values from -60 to 60
- basis_vectors: float32 [16384, 1024], P(('groups', 'row'), ('col', 'sub')), parts along dimension 0, may hold values from -0.0625 to 0.0625
- split_size: int32 [2], P('groups'), parts along dimension 0, may hold values from 256 to 767
Outputs:
- children: float32 [2, 2048, 1024], P('sub', ('groups', 'row'), 'col'), parts along dimension 1
There are 2 independent parts, one for each index of `groups`. A program takes and returns all parts, laid end to end along the dimension named above; each array names one. Nothing has to cross between parts.
Inputs may be any that keep to these rules, and one draw needn't show every extreme that they name: The second subspace has 1024 minus split_size vectors.
All inputs are finite; a program needn't handle non-finite values.
Results may differ from a plain program's by a relative error of at most 0.00011.
Values sent between devices are 32-bit elements; how exact they have to be, the bound alone decides.
No kernel may reach another device: no remote copies, remote signals or barrier semaphores. Data moves between devices by JAX's collectives and lax.ppermute only.
A program may use at most 64 MiB of HBM per device.

v0:
```python
import jax
import jax.numpy as jnp
from jax import lax
from jax.sharding import PartitionSpec as P


def cut_along(array, dim, size):
    before, after = (array.shape[:dim], array.shape[dim + 1 :])
    return jnp.moveaxis(array.reshape(*before, size, -1, *after), dim, 0)


def sent_and_summed(array, axis, dim):
    size = lax.axis_size(axis)
    pieces = lax.all_to_all(cut_along(array, dim, size), axis, 0, 0, tiled=True)
    return jnp.sum(pieces, axis=0)


def copy_for_each(array, axis):
    size = lax.axis_size(axis)
    return lax.all_to_all(
        jnp.broadcast_to(array[None], (size, *array.shape)), axis, 0, 0, tiled=True
    )


def laid_out(pieces, dim):
    dims = list(pieces.shape[1:])
    dims[dim] *= pieces.shape[0]
    return jnp.moveaxis(pieces, 0, dim).reshape(dims)


def gathered_copies(array, axis, dim):
    pieces = copy_for_each(array, axis)
    return laid_out(pieces, dim)


def shards(matrix, basis_vectors, split_size):
    strip = lax.all_gather(basis_vectors, "row", axis=0, tiled=True)
    row_panel = lax.all_to_all(strip, ("col", "sub"), split_axis=0, concat_axis=1, tiled=True)
    partial_image = jnp.dot(
        matrix, row_panel, precision=lax.Precision.HIGHEST, preferred_element_type=jnp.float32
    )
    image = sent_and_summed(partial_image, ("col", "sub"), 1)
    partial_proj = lax.dot_general(
        gathered_copies(basis_vectors, ("col", "sub"), 1),
        image,
        (((0,), (0,)), ((), ())),
        precision=lax.Precision.HIGHEST,
        preferred_element_type=jnp.float32,
    )
    proj_block = sent_and_summed(partial_proj, "row", 0)
    child_block = lax.all_gather(proj_block, "sub", axis=1, tiled=True)
    row_ids = (
        jnp.arange(child_block.shape[0], dtype=jnp.int32)
        + lax.axis_index("row") * child_block.shape[0]
    )
    col_ids = (
        jnp.arange(child_block.shape[1], dtype=jnp.int32)
        + lax.axis_index("col") * child_block.shape[1]
    )
    leading = split_size[0]
    row_first = row_ids < leading
    col_first = col_ids < leading
    mask_one = row_first[:, None] & col_first[None, :]
    mask_two = jnp.logical_not(row_first)[:, None] & jnp.logical_not(col_first)[None, :]
    selected = jnp.where(lax.axis_index("sub") == 0, mask_one, mask_two)
    return jnp.where(selected, child_block, jnp.zeros((), jnp.float32))[None]


def solution(mesh):
    placed = (
        P(("groups", "row"), ("col", "sub")),
        P(("groups", "row"), ("col", "sub")),
        P("groups"),
    )
    return jax.shard_map(
        shards,
        mesh=mesh,
        in_specs=placed,
        out_specs=P("sub", ("groups", "row"), "col"),
        check_vma=False,
    )
```

profile of v0, /device:TPU:33, one launch (start us, length us, event | category | flops | bytes accessed | tf_op | source)
XLA Modules:
  0.0 370.7 jit_solution(7150744775797212419)
XLA Ops:
  6.5 0.0 copy-start
  6.6 0.0 all-gather.2.cloned.1.call-start
  6.6 0.7 all-gather.2.cloned.1.call-update
  7.3 148.1 %all-gather.2.cloned.1.call-done = f32[8192,128]{1,0:T(8,128)} async-done(((f32[256,128]{1,0:T(8,128)}), f32[8192,128]{1,0:T(8,128)}) %all-gather.2.cloned.1.call-update) | async-done | bytes 4194320 | tf_op jit(solution)/shard_map/all_gather | solution.py:37
  155.4 74.3 %all_to_all.34 = f32[8,1024,128]{2,1,0:T(8,128)} all-to-all(f32[8,1024,128]{2,1,0:T(8,128)} %bitcast.30), channel_id=1, replica_groups=mesh['groups'=2,'row'=32,'col'=4,'sub'=2] {'col','sub'}, dimensions={0} | all-to-all | bytes 8388608 | tf_op jit(solution)/shard_map/all_to_all | solution.py:38
  229.7 5.4 %copy.6 = f32[1024,8,128]{0,2,1:T(8,128)} copy(f32[1024,8,128]{2,0,1:T(8,128)} %bitcast.29) | data formatting | bytes 8388608 | tf_op jit(solution)/shard_map/all_to_all | solution.py:38
  235.1 0.0 copy-done
  235.1 0.0 copy-start.1
  235.1 6.3 %fusion.2 = f32[8,256,128]{2,1,0:T(8,128)} fusion(f32[1024,8,128]{0,2,1:T(8,128)} %copy.6, f32[256,1024]{1,0:T(8,128)S(1)} %copy-done), kind=kOutput, calls=%fused_computation.2 | convolution fusion | flops 3221225472 | bytes 6291456 | tf_op jit(solution)/shard_map/dot_general | solution.py:39
  241.4 4.5 %all-to-all-start.1 = ((f32[8,256,128]{2,1,0:T(8,128)}), f32[8,256,128]{2,1,0:T(8,128)S(1)}, u32[]{:S(2)}, u32[]{:S(2)}) async-start(f32[8,256,128]{2,1,0:T(8,128)} %fusion.2), calls=%async_computation.1 | async-start | bytes 2097152 | tf_op jit(solution)/shard_map/all_to_all | solution.py:14
  245.9 0.0 copy-done.1
  245.9 0.1 copy.7
  246.0 15.0 %all-to-all-done.1 = f32[8,256,128]{2,1,0:T(8,128)S(1)} async-done(((f32[8,256,128]{2,1,0:T(8,128)}), f32[8,256,128]{2,1,0:T(8,128)S(1)}, u32[]{:S(2)}, u32[]{:S(2)}) %all-to-all-start.1) | async-done | bytes 1048608 | tf_op jit(solution)/shard_map/all_to_all | solution.py:14
  261.0 1.1 broadcast_in_dim.7
  262.0 4.4 %all-to-all-start.2 = ((f32[8,256,128]{1,2,0:T(8,128)}), f32[8,256,128]{1,2,0:T(8,128)S(1)}, u32[]{:S(2)}, u32[]{:S(2)}) async-start(f32[8,256,128]{1,2,0:T(8,128)} %broadcast_in_dim.7), calls=%async_computation.2 | async-start | bytes 2097152 | tf_op jit(solution)/shard_map/all_to_all | solution.py:20
  266.4 0.1 reduce_sum.18
  266.5 15.0 %all-to-all-done.2 = f32[8,256,128]{1,2,0:T(8,128)S(1)} async-done(((f32[8,256,128]{1,2,0:T(8,128)}), f32[8,256,128]{1,2,0:T(8,128)S(1)}, u32[]{:S(2)}, u32[]{:S(2)}) %all-to-all-start.2) | async-done | bytes 1048608 | tf_op jit(solution)/shard_map/all_to_all | solution.py:20
  281.5 1.2 convolution_bitcast_fusion
  282.7 1.0 copy.8
  283.7 12.6 %all-to-all-start.3 = ((f32[32,32,128]{2,1,0:T(8,128)}), f32[32,32,128]{2,1,0:T(8,128)S(1)}, u32[]{:S(2)}, u32[]{:S(2)}) async-start(f32[32,32,128]{2,1,0:T(8,128)} %bitcast.11), calls=%async_computation.3 | async-start | bytes 1048576 | tf_op jit(solution)/shard_map/all_to_all | solution.py:14
  297.0 63.0 %all-to-all-done.3 = f32[32,32,128]{2,1,0:T(8,128)S(1)} async-done(((f32[32,32,128]{2,1,0:T(8,128)}), f32[32,32,128]{2,1,0:T(8,128)S(1)}, u32[]{:S(2)}, u32[]{:S(2)}) %all-to-all-start.3) | async-done | bytes 524320 | tf_op jit(solution)/shard_map/all_to_all | solution.py:14
  360.1 3.1 all_gather.7
  363.2 0.7 select_bitcast_fusion
  (3 shorter events, 0.1 us)
Async XLA Ops:
  6.5 228.5 %copy-start = (f32[256,1024]{1,0:T(8,128)S(1)}, f32[256,1024]{1,0:T(8,128)}, u32[]{:S(2)}) copy-start(f32[256,1024]{1,0:T(8,128)} %param.3) | copy-start | bytes 3145732
  6.6 148.8 %all-gather.2.cloned.1.call-start = ((), (), s32[]{:S(2)}) async-start(), calls=%async_computation.4 | async-start | bytes 4325376 | tf_op jit(solution)/shard_map/all_gather | solution.py:37
  235.1 10.8 %copy-start.1 = (f32[256,128]{1,0:T(8,128)S(1)}, f32[256,128]{1,0:T(8,128)}, u32[]{:S(2)}) copy-start(f32[256,128]{1,0:T(8,128)} %param.4) | copy-start | bytes 393220
  241.4 19.6 %all-to-all-start.1 = ((f32[8,256,128]{2,1,0:T(8,128)}), f32[8,256,128]{2,1,0:T(8,128)S(1)}, u32[]{:S(2)}, u32[]{:S(2)}) async-start(f32[8,256,128]{2,1,0:T(8,128)} %fusion.2), calls=%async_computation.1 | async-start | bytes 2097152 | tf_op jit(solution)/shard_map/all_to_all | solution.py:14
  262.0 19.5 %all-to-all-start.2 = ((f32[8,256,128]{1,2,0:T(8,128)}), f32[8,256,128]{1,2,0:T(8,128)S(1)}, u32[]{:S(2)}, u32[]{:S(2)}) async-start(f32[8,256,128]{1,2,0:T(8,128)} %broadcast_in_dim.7), calls=%async_computation.2 | async-start | bytes 2097152 | tf_op jit(solution)/shard_map/all_to_all | solution.py:20
  283.7 76.3 %all-to-all-start.3 = ((f32[32,32,128]{2,1,0:T(8,128)}), f32[32,32,128]{2,1,0:T(8,128)S(1)}, u32[]{:S(2)}, u32[]{:S(2)}) async-start(f32[32,32,128]{2,1,0:T(8,128)} %bitcast.11), calls=%async_computation.3 | async-start | bytes 1048576 | tf_op jit(solution)/shard_map/all_to_all | solution.py:14
Sparse Core Ops, SparseCore 0:
  9.4 145.8 all-gather.1
where the time goes:
time: 371 us
  waiting for transfers between devices  242 us (65%)
  blocking collectives  77.4 us (21%)
  starting transfers between devices  21.5 us (6%)
  between operations  14.1 us (4%)
  matrix products  7.56 us (2%)
  local copies, waits for them, and re-layouts  7.52 us (2%)
    all_gather x1, waiting for transfers between devices, shards(): strip = lax.all_gather(basis_vectors, 'row', axis=0, tiled=True)  148 us
    all_to_all x2, waiting for transfers between devices, sent_and_summed(): pieces = lax.all_to_all(cut_along(array, dim, size), axis, 0, 0, tiled=True)  78 us
    all_to_all x1, blocking collectives, shards(): lax.all_to_all(strip, ('col', 'sub'), split_axis=0, concat_axis=1, tiled=...  74.3 us
    all_to_all x2, starting transfers between devices, sent_and_summed(): pieces = lax.all_to_all(cut_along(array, dim, size), axis, 0, 0, tiled=True)  17.1 us
    all_to_all x1, waiting for transfers between devices, copy_for_each(): lax.all_to_all(jnp.broadcast_to(array[None], (size, *array.shape)), axis,...  15 us
  transfers between devices with their start and end apart: 4, of which 4 were waited for; matrix products, arithmetic and copies ran while one was open for 0% of the time, Pallas kernels for 0%

commit v1 on v0

--- a/solution.py
+++ b/solution.py
@@ -34,7 +34,9 @@
 
 
 def shards(matrix, basis_vectors, split_size):
-    strip = lax.all_gather(basis_vectors, "row", axis=0, tiled=True)
+    strip = jnp.concatenate(
+        lax.all_to_all(jnp.stack([basis_vectors] * lax.axis_size("row")), "row", 0, 0), axis=0
+    )
     row_panel = lax.all_to_all(strip, ("col", "sub"), split_axis=0, concat_axis=1, tiled=True)
     partial_image = jnp.dot(
         matrix, row_panel, precision=lax.Precision.HIGHEST, preferred_element_type=jnp.float32

time: 371 us -> 606 us (1.63)
  blocking collectives: 77.4 us -> 477 us
  waiting for transfers between devices: 242 us -> 93 us
  between operations: 14.1 us -> 0.71 us
    all_to_all x0 -> x1, blocking collectives: none -> 420 us  [shards(): lax.all_to_all(jnp.stack([basis_vectors] * lax.axis_size('row')), 'row',...]
    all_gather x1 -> x0, waiting for transfers between devices: 148 us -> none  [shards(): strip = lax.all_gather(basis_vectors, 'row', axis=0, tiled=True)]
    all_to_all x1, blocking collectives: 74.3 us -> 54 us  [shards(): lax.all_to_all(strip, ('col', 'sub'), split_axis=0, concat_axis=1, tiled=...]
  transfers between devices with their start and end apart: 4 -> 3, of which waited for: 4 -> 3; matrix products, arithmetic and copies ran while one was open for 0% -> 0% of each run, Pallas kernels for 0% -> 0%
where the time goes in v1:
time: 606 us; the launch traced here: 605 us
  blocking collectives  477 us (79%)
  waiting for transfers between devices  93 us (15%)
  starting transfers between devices  16.8 us (3%)
  local copies, waits for them, and re-layouts  8.96 us (1%)
  matrix products  7.58 us (1%)
    all_to_all x1, blocking collectives, shards(): lax.all_to_all(jnp.stack([basis_vectors] * lax.axis_size('row')), 'row',...  420 us
    all_to_all x2, waiting for transfers between devices, sent_and_summed(): pieces = lax.all_to_all(cut_along(array, dim, size), axis, 0, 0, tiled=True)  78 us
    all_to_all x1, blocking collectives, shards(): lax.all_to_all(strip, ('col', 'sub'), split_axis=0, concat_axis=1, tiled=...  54 us
    all_to_all x1, waiting for transfers between devices, copy_for_each(): lax.all_to_all(jnp.broadcast_to(array[None], (size, *array.shape)), axis,...  15 us
    all_to_all x2, starting transfers between devices, sent_and_summed(): pieces = lax.all_to_all(cut_along(array, dim, size), axis, 0, 0, tiled=True)  12.4 us
  transfers between devices with their start and end apart: 3, of which 3 were waited for; matrix products, arithmetic and copies ran while one was open for 0% of the time, Pallas kernels for 0%

profile of v1, /device:TPU:33, one launch (start us, length us, event | category | flops | bytes accessed | tf_op | source)
XLA Modules:
  0.0 605.2 jit_solution(3029789306048276531)
XLA Ops:
  0.0 0.0 copy-start
  0.0 1.5 stack.2
  1.5 420.2 %all_to_all.39 = f32[32,256,128]{2,1,0:T(8,128)S(1)} all-to-all(f32[32,256,128]{2,1,0:T(8,128)S(1)} %stack.2), channel_id=1, replica_groups=mesh['groups'=2,'row'=32,'col'=4,'sub'=2] {'row'}, dimensions={0} | all-to-all | bytes 8388608 | tf_op jit(solution)/shard_map/all_to_all | solution.py:38
  421.7 54.0 %all_to_all.40 = f32[8,1024,128]{2,1,0:T(8,128)} all-to-all(f32[8,1024,128]{2,1,0:T(8,128)S(1)} %bitcast.29), channel_id=1, replica_groups=mesh['groups'=2,'row'=32,'col'=4,'sub'=2] {'col','sub'}, dimensions={0} | all-to-all | bytes 8388608 | tf_op jit(solution)/shard_map/all_to_all | solution.py:40
  475.7 5.3 copy.6
  481.0 0.0 copy-done
  481.0 0.0 copy-start.1
  481.0 6.3 %fusion.2 = f32[8,256,128]{2,1,0:T(8,128)} fusion(f32[1024,8,128]{0,2,1:T(8,128)} %copy.6, f32[256,1024]{1,0:T(8,128)S(1)} %copy-done), kind=kOutput, calls=%fused_computation.2 | convolution fusion | flops 3221225472 | bytes 6291456 | tf_op jit(solution)/shard_map/dot_general | solution.py:41
  487.4 4.5 all-to-all-start.2
  491.9 0.0 copy-done.1
  491.9 0.1 copy.7
  492.0 15.0 %all-to-all-done.2 = f32[8,256,128]{2,1,0:T(8,128)S(1)} async-done(((f32[8,256,128]{2,1,0:T(8,128)}), f32[8,256,128]{2,1,0:T(8,128)S(1)}, u32[]{:S(2)}, u32[]{:S(2)}) %all-to-all-start.2) | async-done | bytes 1048608 | tf_op jit(solution)/shard_map/all_to_all | solution.py:14
  507.0 1.1 broadcast_in_dim.7
  508.0 4.4 all-to-all-start.3
  512.4 0.1 reduce_sum.18
  512.5 15.0 %all-to-all-done.3 = f32[8,256,128]{1,2,0:T(8,128)S(1)} async-done(((f32[8,256,128]{1,2,0:T(8,128)}), f32[8,256,128]{1,2,0:T(8,128)S(1)}, u32[]{:S(2)}, u32[]{:S(2)}) %all-to-all-start.3) | async-done | bytes 1048608 | tf_op jit(solution)/shard_map/all_to_all | solution.py:20
  527.5 1.2 convolution_bitcast_fusion
  528.7 1.0 copy.8
  529.7 7.8 %all-to-all-start.4 = ((f32[32,32,128]{2,1,0:T(8,128)}), f32[32,32,128]{2,1,0:T(8,128)S(1)}, u32[]{:S(2)}, u32[]{:S(2)}) async-start(f32[32,32,128]{2,1,0:T(8,128)} %bitcast.11), calls=%async_computation.4 | async-start | bytes 1048576 | tf_op jit(solution)/shard_map/all_to_all | solution.py:14
  538.3 63.0 %all-to-all-done.4 = f32[32,32,128]{2,1,0:T(8,128)S(1)} async-done(((f32[32,32,128]{2,1,0:T(8,128)}), f32[32,32,128]{2,1,0:T(8,128)S(1)}, u32[]{:S(2)}, u32[]{:S(2)}) %all-to-all-start.4) | async-done | bytes 524320 | tf_op jit(solution)/shard_map/all_to_all | solution.py:14
  601.4 3.1 all_gather.3
  604.5 0.7 select_bitcast_fusion
  (3 shorter events, 0.1 us)
Async XLA Ops:
  0.0 481.0 %copy-start = (f32[256,1024]{1,0:T(8,128)S(1)}, f32[256,1024]{1,0:T(8,128)}, u32[]{:S(2)}) copy-start(f32[256,1024]{1,0:T(8,128)} %param.3) | copy-start | bytes 3145732
  481.0 10.9 %copy-start.1 = (f32[256,128]{1,0:T(8,128)S(1)}, f32[256,128]{1,0:T(8,128)}, u32[]{:S(2)}) copy-start(f32[256,128]{1,0:T(8,128)} %param.4) | copy-start | bytes 393220
  487.4 19.6 %all-to-all-start.2 = ((f32[8,256,128]{2,1,0:T(8,128)}), f32[8,256,128]{2,1,0:T(8,128)S(1)}, u32[]{:S(2)}, u32[]{:S(2)}) async-start(f32[8,256,128]{2,1,0:T(8,128)} %fusion.2), calls=%async_computation.2 | async-start | bytes 2097152 | tf_op jit(solution)/shard_map/all_to_all | solution.py:14
  508.0 19.5 %all-to-all-start.3 = ((f32[8,256,128]{1,2,0:T(8,128)}), f32[8,256,128]{1,2,0:T(8,128)S(1)}, u32[]{:S(2)}, u32[]{:S(2)}) async-start(f32[8,256,128]{1,2,0:T(8,128)} %broadcast_in_dim.7), calls=%async_computation.3 | async-start | bytes 2097152 | tf_op jit(solution)/shard_map/all_to_all | solution.py:20
  529.7 71.6 %all-to-all-start.4 = ((f32[32,32,128]{2,1,0:T(8,128)}), f32[32,32,128]{2,1,0:T(8,128)S(1)}, u32[]{:S(2)}, u32[]{:S(2)}) async-start(f32[32,32,128]{2,1,0:T(8,128)} %bitcast.11), calls=%async_computation.4 | async-start | bytes 1048576 | tf_op jit(solution)/shard_map/all_to_all | solution.py:14

commit v2 on v0

--- a/solution.py
+++ b/solution.py
@@ -35,7 +35,12 @@
 
 def shards(matrix, basis_vectors, split_size):
     strip = lax.all_gather(basis_vectors, "row", axis=0, tiled=True)
-    row_panel = lax.all_to_all(strip, ("col", "sub"), split_axis=0, concat_axis=1, tiled=True)
+    row_panel = jnp.concatenate(
+        lax.all_to_all(
+            jnp.stack(jnp.split(strip, lax.axis_size(("col", "sub")), axis=0)), ("col", "sub"), 0, 0
+        ),
+        axis=1,
+    )
     partial_image = jnp.dot(
         matrix, row_panel, precision=lax.Precision.HIGHEST, preferred_element_type=jnp.float32
     )

time: 371 us -> 371 us (level)
  blocking collectives: 77.4 us -> 95.4 us
  waiting for transfers between devices: 242 us -> 225 us
  local copies, waits for them, and re-layouts: 7.52 us -> 12.4 us
  starting transfers between devices: 21.5 us -> 17.1 us
    all_to_all x1 -> x2, blocking collectives: 74.3 us -> 92.3 us  [the longest x1 73.8 us: shards(): lax.all_to_all(jnp.stack(jnp.split(strip, lax.axis_size(('col', 'sub')),...]
    all_to_all x2 -> x1, waiting for transfers between devices: 78 us -> 63 us  [sent_and_summed(): pieces = lax.all_to_all(cut_along(array, dim, size), axis, 0, 0, tiled=True)]
    unnamed x5 -> x12, local copies, waits for them, and re-layouts: 0.1 us -> 9.28 us
    all_to_all x1 -> x0, local copies, waits for them, and re-layouts: 5.37 us -> none  [shards(): lax.all_to_all(strip, ('col', 'sub'), split_axis=0, concat_axis=1, tiled=...]
    all_to_all x2 -> x1, starting transfers between devices: 17.1 us -> 12.6 us  [sent_and_summed(): pieces = lax.all_to_all(cut_along(array, dim, size), axis, 0, 0, tiled=True)]
  transfers between devices with their start and end apart: 4 -> 3, of which waited for: 4 -> 3; matrix products, arithmetic and copies ran while one was open for 0% -> 0% of each run, Pallas kernels for 0% -> 0%
where the time goes in v2:
time: 371 us; the launch traced here: 370 us
  waiting for transfers between devices  225 us (61%)
  blocking collectives  95.4 us (26%)
  starting transfers between devices  17.1 us (5%)
  between operations  14.2 us (4%)
  local copies, waits for them, and re-layouts  12.4 us (3%)
  matrix products  4.67 us (1%)
    all_gather x1, waiting for transfers between devices, shards(): strip = lax.all_gather(basis_vectors, 'row', axis=0, tiled=True)  147 us
    all_to_all x1, blocking collectives, shards(): lax.all_to_all(jnp.stack(jnp.split(strip, lax.axis_size(('col', 'sub')),...  73.8 us
    all_to_all x1, waiting for transfers between devices, sent_and_summed(): pieces = lax.all_to_all(cut_along(array, dim, size), axis, 0, 0, tiled=True)  63 us
    all_to_all x1, blocking collectives, sent_and_summed(): pieces = lax.all_to_all(cut_along(array, dim, size), axis, 0, 0, tiled=True)  18.5 us
    all_to_all x1, waiting for transfers between devices, copy_for_each(): lax.all_to_all(jnp.broadcast_to(array[None], (size, *array.shape)), axis,...  15 us
    all_to_all x1, starting transfers between devices, sent_and_summed(): pieces = lax.all_to_all(cut_along(array, dim, size), axis, 0, 0, tiled=True)  12.6 us
    unnamed x12, local copies, waits for them, and re-layouts  9.28 us
  transfers between devices with their start and end apart: 3, of which 3 were waited for; matrix products, arithmetic and copies ran while one was open for 0% of the time, Pallas kernels for 0%

profile of v2, /device:TPU:33, one launch (start us, length us, event | category | flops | bytes accessed | tf_op | source)
XLA Modules:
  0.0 369.8 jit_solution(2510449901732508686)
XLA Ops:
  6.5 0.0 copy-start
  6.6 0.0 all-gather.2.cloned.1.call-start
  6.6 1.7 copy.7
  8.3 0.1 all-gather.2.cloned.1.call-update
  8.3 147.1 %all-gather.2.cloned.1.call-done = f32[8192,128]{0,1:T(8,128)} async-done(((f32[256,128]{0,1:T(8,128)}), f32[8192,128]{0,1:T(8,128)}) %all-gather.2.cloned.1.call-update) | async-done | bytes 4194320 | tf_op jit(solution)/shard_map/all_gather | solution.py:37
  155.5 1.1 fusion.7
  156.5 1.1 fusion.6
  157.6 1.1 fusion.5
  158.7 1.1 fusion.4
  159.8 1.1 fusion.3
  160.9 1.1 fusion.2
  162.0 1.1 fusion.1
  163.0 1.1 fusion
  164.1 73.8 %all_to_all.20 = f32[8,1024,128]{1,2,0:T(8,128)S(1)} all-to-all(f32[8,1024,128]{1,2,0:T(8,128)S(1)} %fusion), channel_id=1, replica_groups=mesh['groups'=2,'row'=32,'col'=4,'sub'=2] {'col','sub'}, dimensions={0} | all-to-all | bytes 8388608 | tf_op jit(solution)/shard_map/all_to_all | solution.py:39
  238.0 0.0 copy-done
  238.0 0.0 copy-start.1
  238.0 3.5 fusion.10
  241.4 18.5 %all_to_all.21 = f32[8,256,128]{1,2,0:T(8,128)S(1)} all-to-all(f32[8,256,128]{1,2,0:T(8,128)S(1)} %bitcast.57), channel_id=1, replica_groups=mesh['groups'=2,'row'=32,'col'=4,'sub'=2] {'col','sub'}, dimensions={0} | all-to-all | bytes 2097152 | tf_op jit(solution)/shard_map/all_to_all | solution.py:14
  259.9 0.0 copy-done.1
  259.9 1.1 broadcast_in_dim.7
  261.0 4.5 %all-to-all-start.2 = ((f32[8,256,128]{1,2,0:T(8,128)}), f32[8,256,128]{1,2,0:T(8,128)S(1)}, u32[]{:S(2)}, u32[]{:S(2)}) async-start(f32[8,256,128]{1,2,0:T(8,128)} %broadcast_in_dim.7), calls=%async_computation.2 | async-start | bytes 2097152 | tf_op jit(solution)/shard_map/all_to_all | solution.py:20
  265.5 0.1 reduce_sum.18
  265.6 15.0 %all-to-all-done.2 = f32[8,256,128]{1,2,0:T(8,128)S(1)} async-done(((f32[8,256,128]{1,2,0:T(8,128)}), f32[8,256,128]{1,2,0:T(8,128)S(1)}, u32[]{:S(2)}, u32[]{:S(2)}) %all-to-all-start.2) | async-done | bytes 1048608 | tf_op jit(solution)/shard_map/all_to_all | solution.py:20
  280.6 1.2 convolution_bitcast_fusion
  281.8 1.0 copy.9
  282.8 12.6 %all-to-all-start.3 = ((f32[32,32,128]{2,1,0:T(8,128)}), f32[32,32,128]{2,1,0:T(8,128)S(1)}, u32[]{:S(2)}, u32[]{:S(2)}) async-start(f32[32,32,128]{2,1,0:T(8,128)} %bitcast.17), calls=%async_computation.3 | async-start | bytes 1048576 | tf_op jit(solution)/shard_map/all_to_all | solution.py:14
  296.1 63.0 %all-to-all-done.3 = f32[32,32,128]{2,1,0:T(8,128)S(1)} async-done(((f32[32,32,128]{2,1,0:T(8,128)}), f32[32,32,128]{2,1,0:T(8,128)S(1)}, u32[]{:S(2)}, u32[]{:S(2)}) %all-to-all-start.3) | async-done | bytes 524320 | tf_op jit(solution)/shard_map/all_to_all | solution.py:14
  359.2 3.1 all_gather.7
  362.3 0.7 select_bitcast_fusion
  (3 shorter events, 0.1 us)
Async XLA Ops:
  6.5 231.4 %copy-start = (f32[256,1024]{1,0:T(8,128)S(1)}, f32[256,1024]{1,0:T(8,128)}, u32[]{:S(2)}) copy-start(f32[256,1024]{1,0:T(8,128)} %param.3) | copy-start | bytes 3145732
  6.6 148.9 %all-gather.2.cloned.1.call-start = ((), (), s32[]{:S(2)}) async-start(), calls=%async_computation.4 | async-start | bytes 4325376 | tf_op jit(solution)/shard_map/all_gather | solution.py:37
  238.0 22.0 %copy-start.1 = (f32[256,128]{0,1:T(8,128)S(1)}, f32[256,128]{0,1:T(8,128)}, u32[]{:S(2)}) copy-start(f32[256,128]{0,1:T(8,128)} %copy.7) | copy-start | bytes 393220
  261.0 19.6 %all-to-all-start.2 = ((f32[8,256,128]{1,2,0:T(8,128)}), f32[8,256,128]{1,2,0:T(8,128)S(1)}, u32[]{:S(2)}, u32[]{:S(2)}) async-start(f32[8,256,128]{1,2,0:T(8,128)} %broadcast_in_dim.7), calls=%async_computation.2 | async-start | bytes 2097152 | tf_op jit(solution)/shard_map/all_to_all | solution.py:20
  282.8 76.4 %all-to-all-start.3 = ((f32[32,32,128]{2,1,0:T(8,128)}), f32[32,32,128]{2,1,0:T(8,128)S(1)}, u32[]{:S(2)}, u32[]{:S(2)}) async-start(f32[32,32,128]{2,1,0:T(8,128)} %bitcast.17), calls=%async_computation.3 | async-start | bytes 1048576 | tf_op jit(solution)/shard_map/all_to_all | solution.py:14
Sparse Core Ops, SparseCore 0:
  9.4 145.9 all-gather.1
